TPU v7x, 128 devices: a whole 4x4x4 slice. The times are simulated.
128 devices in a mesh: ep: 32 (over z, x, core), dp: 4 (over y).
Axes of the slice: x: 4, y: 4, z: 4, core: 2. Of those that a mesh axis runs over, the one named last changes fastest.
Arguments:
- grad_out: float32 [16384, 1536], P(('ep', 'dp')), may hold values from -6 to 6
- tokens: bfloat16 [16384, 1536], P(('ep', 'dp')), may hold values from -6 to 6
- probs: float32 [16384, 4], P(('ep', 'dp')), may hold values from 0.1 to 0.5
- expert_ids: int32 [16384, 4], P(('ep', 'dp')), may hold values from 0 to 31, all different within a row; in each aligned block of 128 rows (0 to 127, 128 to 255, ...) at most 20 rows name the same one
- priority: int32 [128, 128], P(('ep', 'dp')), may hold values from 0 to 127, each once within a row
- cap_counts: int32 [32], replicated, may hold values from 10 to 20, as said below
- gate_weight: bfloat16 [32, 1536, 1536], P('ep'), may hold values from -0.15625 to 0.15625
- up_weight: bfloat16 [32, 1536, 1536], P('ep'), may hold values from -0.15625 to 0.15625
- down_weight: bfloat16 [32, 1536, 1536], P('ep'), may hold values from -0.15625 to 0.15625
Outputs:
- input_grad: bfloat16 [16384, 1536], P(('ep', 'dp'))
- prob_grad: float32 [16384, 4], P(('ep', 'dp'))
- gate_grad: bfloat16 [32, 1536, 1536], P('ep', 'dp')
- up_grad: bfloat16 [32, 1536, 1536], P('ep', 'dp')
- down_grad: bfloat16 [32, 1536, 1536], P('ep', 'dp')
Inputs may be any that keep to these rules, and one draw needn't show every extreme that they name: `expert_ids`: each row names 4 different experts; among the rows of one device no expert is named by more than 20 rows, and in some device some expert is named by exactly 20 rows. `priority`: each row orders the 128 tokens of one device, each number once. `cap_counts`: some expert has exactly 20.
All inputs are finite; a program needn't handle non-finite values. Where the computation divides by a largest or mean magnitude, that divisor is 1e-20 or more.
Results may differ from a plain program's by a relative error of at most 0.017.
Values may be sent and summed in bfloat16 or wider, within the bound.
A program may use at most 128 MiB of HBM per device.

v0:
```python
import jax
import jax.numpy as jnp
from jax import lax
from jax.sharding import PartitionSpec as P

sharpness = 1.702


def contract_last(first_op, second_op):
    return lax.dot_general(
        first_op, second_op, (((1,), (1,)), ((), ())), preferred_element_type=jnp.float32
    )


def contract_first(first_op, second_op):
    return lax.dot_general(
        first_op, second_op, (((0,), (0,)), ((), ())), preferred_element_type=jnp.float32
    )


def route_table(expert_ids, priority, cap_counts, buckets, capacity):
    ranking = priority[0]
    earlier = (ranking[None, :] < ranking[:, None]).astype(jnp.float32)
    expert_range = lax.broadcasted_iota(jnp.int32, (1, 1, buckets), 2)
    matches = (expert_ids[:, :, None] == expert_range).astype(jnp.float32)
    routed = jnp.sum(matches, axis=1)
    before = jnp.dot(earlier, routed)
    slot_rank = jnp.sum(matches * before[:, None, :], axis=2)
    keep_limit = jnp.sum(matches * cap_counts.astype(jnp.float32)[None, None, :], axis=2)
    slot_range = lax.broadcasted_iota(jnp.float32, (1, 1, capacity), 2)
    slot_hit = (
        (slot_rank[:, :, None] == slot_range) & (slot_rank < keep_limit)[:, :, None]
    ).astype(jnp.float32)
    placement = matches[:, :, :, None] * slot_hit[:, :, None, :]
    return placement.reshape(expert_ids.shape[0], expert_ids.shape[1], buckets * capacity)


def deltas(slot_x, slot_g, w_gate, w_up, w_down):
    gate_pre = contract_last(slot_x, w_gate)
    up_pre = contract_last(slot_x, w_up)
    act_delta = contract_last(slot_g, w_down)
    squash = jax.nn.sigmoid(sharpness * gate_pre)
    gated = gate_pre * squash
    activated = (up_pre + 1.0) * gated
    up_delta = (act_delta * gated).astype(jnp.bfloat16)
    gate_delta = (
        act_delta * (up_pre + 1.0) * (squash + sharpness * gate_pre * squash * (1.0 - squash))
    ).astype(jnp.bfloat16)
    return (activated, act_delta, gate_delta, up_delta)


def on_device(
    grad_out, tokens, probs, expert_ids, priority, cap_counts, gate_weight, up_weight, down_weight
):
    ep_size = lax.axis_size("ep")
    dp_size = lax.axis_size("dp")
    tok_rows, model_width = tokens.shape
    route_count = expert_ids.shape[1]
    capacity = 5 * route_count * tok_rows // (4 * ep_size)
    slot_rows = ep_size * capacity
    placement = route_table(expert_ids, priority, cap_counts, ep_size, capacity)
    slot_table = jnp.sum(placement, axis=1)
    table_low = slot_table.astype(jnp.bfloat16)
    row_scale = jnp.maximum(jnp.max(jnp.abs(grad_out), axis=1), 1.0)
    quantized = (grad_out / row_scale[:, None]).astype(jnp.bfloat16)
    send_prob = jnp.sum(placement * probs[:, :, None], axis=(0, 1))
    send_scale = jnp.sum(slot_table * row_scale[:, None], axis=0)
    send_x = jnp.einsum("ts,td->sd", table_low, tokens, preferred_element_type=jnp.float32).astype(
        jnp.bfloat16
    )
    send_g = (
        jnp.einsum("ts,td->sd", table_low, quantized, preferred_element_type=jnp.float32)
        * (send_prob * send_scale)[:, None]
    ).astype(jnp.bfloat16)
    bucket_shape = (ep_size, capacity, model_width)

    def exchange(a):
        return lax.all_to_all(a, "ep", split_axis=0, concat_axis=0, tiled=True)

    slot_x = exchange(send_x.reshape(bucket_shape)).reshape(slot_rows, model_width)
    all_x = lax.all_gather(slot_x, "dp", axis=0, tiled=True)
    slot_g = exchange(send_g.reshape(bucket_shape)).reshape(slot_rows, model_width)
    all_g = lax.all_gather(slot_g, "dp", axis=0, tiled=True)
    w_gate = gate_weight[0]
    w_up = up_weight[0]
    w_down = down_weight[0]
    activated, act_delta, gate_delta, up_delta = deltas(slot_x, slot_g, w_gate, w_up, w_down)
    slot_in = (
        jnp.dot(gate_delta, w_gate, preferred_element_type=jnp.float32)
        + jnp.dot(up_delta, w_up, preferred_element_type=jnp.float32)
    ).astype(jnp.bfloat16)
    slot_out = jnp.sum(activated * act_delta, axis=1)
    back_in = exchange(slot_in.reshape(bucket_shape))
    back_prob = exchange(slot_out.reshape(ep_size, capacity).astype(jnp.bfloat16))
    prob_grad = jnp.einsum("tks,s->tk", placement, back_prob.reshape(slot_rows)) / probs
    input_grad = jnp.einsum(
        "ts,sd->td",
        table_low,
        back_in.reshape(slot_rows, model_width),
        preferred_element_type=jnp.float32,
    ).astype(jnp.bfloat16)
    share = w_gate.shape[0] // dp_size
    first = lax.axis_index("dp") * share

    def mine(w):
        return lax.dynamic_slice_in_dim(w, first, share, 0)

    act_mine, _, gd_mine, ud_mine = deltas(all_x, all_g, mine(w_gate), mine(w_up), mine(w_down))
    gate_share = contract_first(gd_mine, all_x).astype(jnp.bfloat16)
    up_share = contract_first(ud_mine, all_x).astype(jnp.bfloat16)
    down_share = contract_first(act_mine.astype(jnp.bfloat16), all_g).astype(jnp.bfloat16)
    return (input_grad, prob_grad, gate_share[None], up_share[None], down_share[None])


def solution(mesh):
    return jax.shard_map(
        on_device,
        mesh=mesh,
        in_specs=(
            P(("ep", "dp"), None),
            P(("ep", "dp"), None),
            P(("ep", "dp"), None),
            P(("ep", "dp"), None),
            P(("ep", "dp"), None),
            P(),
            P("ep", None, None),
            P("ep", None, None),
            P("ep", None, None),
        ),
        out_specs=(
            P(("ep", "dp"), None),
            P(("ep", "dp"), None),
            P("ep", "dp", None),
            P("ep", "dp", None),
            P("ep", "dp", None),
        ),
        check_vma=False,
    )
```

profile of v0, /device:TPU:1, one launch (start us, length us, event | category | flops | bytes accessed | tf_op | source)
XLA Modules:
  0.0 248.0 jit_solution(7221112332950681031)
XLA Ops:
  13.6 1.9 convolution_convert_fusion
  15.6 2.5 reshape.94
  18.0 40.7 %all_to_all.24 = bf16[32,20,1536]{2,1,0:T(8,128)(2,1)} all-to-all(bf16[32,20,1536]{2,1,0:T(8,128)(2,1)S(1)} %reshape.94), channel_id=1, replica_groups=mesh['ep'=32,'dp'=4] {'ep'}, dimensions={0} | all-to-all | bytes 3932160 | tf_op jit(solution)/shard_map/all_to_all | solution.py:78
  58.7 4.1 %reshape.95 = bf16[640,1536]{1,0:T(8,128)(2,1)} reshape(bf16[32,20,1536]{2,1,0:T(8,128)(2,1)} %all_to_all.24) | data formatting | bytes 3932160 | tf_op jit(solution)/shard_map/reshape | solution.py:80
  63.1 2.1 multiply_convert_fusion.5
  65.2 2.5 reshape.92
  67.6 35.0 %all_to_all.25 = bf16[32,20,1536]{2,1,0:T(8,128)(2,1)} all-to-all(bf16[32,20,1536]{2,1,0:T(8,128)(2,1)S(1)} %reshape.92), channel_id=1, replica_groups=mesh['ep'=32,'dp'=4] {'ep'}, dimensions={0} | all-to-all | bytes 3932160 | tf_op jit(solution)/shard_map/all_to_all | solution.py:78
  102.6 4.1 %reshape.93 = bf16[640,1536]{1,0:T(8,128)(2,1)} reshape(bf16[32,20,1536]{2,1,0:T(8,128)(2,1)} %all_to_all.25) | data formatting | bytes 3932160 | tf_op jit(solution)/shard_map/reshape | solution.py:82
  106.8 5.3 %fusion.6 = f32[640,1536]{1,0:T(8,128)S(1)} fusion(bf16[640,1536]{1,0:T(8,128)(2,1)S(1)} %copy-done.2, bf16[1,1536,1536]{2,1,0:T(8,128)(2,1)} %param.16), kind=kOutput, calls=%fused_computation.6 | convolution fusion | flops 3019898880 | bytes 10616832 | tf_op jit(solution)/shard_map/dot_general | solution.py:10
  112.1 6.6 %fusion.2 = f32[640,1536]{1,0:T(8,128)S(1)} fusion(bf16[640,1536]{1,0:T(8,128)(2,1)S(1)} %copy-done.2, bf16[1,1536,1536]{2,1,0:T(8,128)(2,1)} %param.15), kind=kOutput, calls=%fused_computation.2 | convolution fusion | flops 3019898880 | bytes 10616832 | tf_op jit(solution)/shard_map/dot_general | solution.py:10
  118.8 5.4 %multiply_reduce_fusion = (bf16[640]{0:T(1024)(128)(2,1)S(1)}, f32[640,1536]{1,0:T(8,128)}) fusion(f32[640,1536]{1,0:T(8,128)S(1)} %fusion.6, f32[640,1536]{1,0:T(8,128)S(1)} %fusion.2, bf16[640,1536]{1,0:T(8,128)(2,1)S(1)} %copy-done.3, bf16[1,1536,1536]{2,1,0:T(8,128)(2,1)S(1)} %bitcast.64), kind=kOutput, calls=%fused_computation.15 | convolution fusion | flops 3028745728 | bytes 18482432 | tf_op jit(solution)/shard_map/dot_general | solution.py:10
  124.9 3.8 %all-to-all-start.3 = ((bf16[32,1,20]{2,1,0:T(2,128)(2,1)}), bf16[32,1,20]{2,1,0:T(2,128)(2,1)S(1)}, u32[]{:S(2)}, u32[]{:S(2)}) async-start(bf16[32,1,20]{2,1,0:T(2,128)(2,1)} %convert_element_type.97), calls=%async_computation.3 | async-start | bytes 32768 | tf_op jit(solution)/shard_map/all_to_all | solution.py:78
  128.8 8.9 %fusion = f32[640,1536]{1,0:T(8,128)S(1)} fusion(bf16[1,1536,1536]{2,1,0:T(8,128)(2,1)} %param.15, f32[640,1536]{1,0:T(8,128)} %get-tuple-element.12, f32[640,1536]{1,0:T(8,128)} %copy-done.9, f32[640,1536]{1,0:T(8,128)} %copy-done.11), kind=kOutput, calls=%fused_computation | convolution fusion | flops 3031695360 | bytes 20447232 | tf_op jit(solution)/shard_map/dot_general | solution.py:89
  137.7 5.8 %add_convert_fusion = bf16[640,1536]{1,0:T(8,128)(2,1)S(1)} fusion(f32[640,1536]{1,0:T(8,128)S(1)} %fusion, bf16[1,1536,1536]{2,1,0:T(8,128)(2,1)} %param.16, f32[640,1536]{1,0:T(8,128)S(1)} %copy-done.13, f32[640,1536]{1,0:T(8,128)S(1)} %copy-done.10), kind=kOutput, calls=%fused_computation.16 | convolution fusion | flops 3028746240 | bytes 18481152 | tf_op jit(solution)/shard_map/dot_general | solution.py:90
  143.6 2.1 reshape.96
  145.7 7.3 %all-to-all-start.2 = ((bf16[32,20,1536]{2,1,0:T(8,128)(2,1)}), bf16[32,20,1536]{2,1,0:T(8,128)(2,1)S(1)}, u32[]{:S(2)}, u32[]{:S(2)}) async-start(bf16[32,20,1536]{2,1,0:T(8,128)(2,1)} %reshape.96), calls=%async_computation.2 | async-start | bytes 4718592 | tf_op jit(solution)/shard_map/all_to_all | solution.py:78
  154.0 30.6 %all-to-all-done.2 = bf16[32,20,1536]{2,1,0:T(8,128)(2,1)S(1)} async-done(((bf16[32,20,1536]{2,1,0:T(8,128)(2,1)}), bf16[32,20,1536]{2,1,0:T(8,128)(2,1)S(1)}, u32[]{:S(2)}, u32[]{:S(2)}) %all-to-all-start.2) | async-done | bytes 1966112 | tf_op jit(solution)/shard_map/all_to_all | solution.py:78
  186.1 9.9 %fusion.25 = f32[2560,384]{1,0:T(8,128)} fusion(bf16[2560,1536]{1,0:T(8,128)(2,1)} %all-gather.5.cloned.1.call-done, bf16[1,1536,1536]{2,1,0:T(8,128)(2,1)} %param.15, s32[]{:T(128)S(6)} %select_n.2), kind=kOutput, calls=%fused_computation.41 | convolution fusion | flops 3019898880 | bytes 12976132 | tf_op jit(solution)/shard_map/dot_general | solution.py:10
  196.0 7.5 %convolution_add_fusion = f32[2560,384]{1,0:T(8,128)} fusion(bf16[2560,1536]{1,0:T(8,128)(2,1)S(1)} %copy-done.6, bf16[1,1536,1536]{2,1,0:T(8,128)(2,1)} %param.16, s32[]{:T(128)S(6)} %select_n.2), kind=kOutput, calls=%fused_computation.10 | convolution fusion | flops 3020881920 | bytes 12976132 | tf_op jit(solution)/shard_map/dot_general | solution.py:10
  203.4 16.9 %all-gather.3.cloned.1.call-done = bf16[2560,1536]{1,0:T(8,128)(2,1)} async-done(((bf16[640,1536]{1,0:T(8,128)(2,1)}), bf16[2560,1536]{1,0:T(8,128)(2,1)}) %all-gather.3.cloned.1.call-update) | async-done | bytes 7864336 | tf_op jit(solution)/shard_map/all_gather | solution.py:83
  220.3 7.4 %fusion.28 = f32[2560,384]{1,0:T(8,128)S(1)} fusion(bf16[2560,1536]{1,0:T(8,128)(2,1)} %all-gather.3.cloned.1.call-done, bf16[1,1536,1536]{2,1,0:T(8,128)(2,1)} %param.17, s32[]{:T(128)S(6)} %select_n.2), kind=kOutput, calls=%fused_computation.44 | convolution fusion | flops 3019898880 | bytes 12976132 | tf_op jit(solution)/shard_map/dot_general | solution.py:10
  227.7 4.4 %fusion.15 = bf16[1,384,1536]{2,1,0:T(8,128)(2,1)} fusion(bf16[2560,1536]{1,0:T(8,128)(2,1)S(1)} %copy-done.7, f32[2560,384]{1,0:T(8,128)S(1)} %fusion.28, f32[2560,384]{1,0:T(8,128)S(1)} %copy-done.8), kind=kOutput, calls=%fused_computation.28 | convolution fusion | flops 3027369984 | bytes 16908288 | tf_op jit(solution)/shard_map/dot_general | solution.py:16
  232.2 4.5 %fusion.14 = bf16[1,384,1536]{2,1,0:T(8,128)(2,1)} fusion(bf16[2560,1536]{1,0:T(8,128)(2,1)S(1)} %copy-done.7, f32[2560,384]{1,0:T(8,128)S(1)} %fusion.28, f32[2560,384]{1,0:T(8,128)S(1)} %copy-done.12, f32[2560,384]{1,0:T(8,128)S(1)} %copy-done.8), kind=kOutput, calls=%fused_computation.27 | convolution fusion | flops 3031302144 | bytes 20840448 | tf_op jit(solution)/shard_map/dot_general | solution.py:16
  236.7 4.4 %fusion.16 = bf16[1,384,1536]{2,1,0:T(8,128)(2,1)} fusion(bf16[2560,1536]{1,0:T(8,128)(2,1)S(1)} %bitcast.62, f32[2560,384]{1,0:T(8,128)S(1)} %copy-done.12, f32[2560,384]{1,0:T(8,128)S(1)} %copy-done.8), kind=kOutput, calls=%fused_computation.29 | convolution fusion | flops 3027369984 | bytes 16908288 | tf_op jit(solution)/shard_map/dot_general | solution.py:16
  (65 shorter events, 9.9 us)
Async XLA Ops:
  7.2 6.5 %copy-start = (bf16[128,1536]{1,0:T(8,128)(2,1)S(1)}, bf16[128,1536]{1,0:T(8,128)(2,1)}, u32[]{:S(2)}) copy-start(bf16[128,1536]{1,0:T(8,128)(2,1)} %param.10) | copy-start | bytes 1179652
  7.2 178.9 %all-gather.5.cloned.1.call-start = ((), (), s32[]{:S(2)}) async-start(), calls=%async_computation.5 | async-start | bytes 9830400 | tf_op jit(solution)/shard_map/all_gather | solution.py:81
  58.7 4.3 %copy-start.4 = (f32[128,1536]{1,0:T(8,128)S(1)}, f32[128,1536]{1,0:T(8,128)}, u32[]{:S(2)}) copy-start(f32[128,1536]{1,0:T(8,128)} %param.9) | copy-start | bytes 2359300
  62.8 157.5 %all-gather.3.cloned.1.call-start = ((), (), s32[]{:S(2)}) async-start(), calls=%async_computation.4 | async-start | bytes 9830400 | tf_op jit(solution)/shard_map/all_gather | solution.py:83
  102.6 4.2 %copy-start.2 = (bf16[640,1536]{1,0:T(8,128)(2,1)S(1)}, bf16[640,1536]{1,0:T(8,128)(2,1)}, u32[]{:S(2)}) copy-start(bf16[640,1536]{1,0:T(8,128)(2,1)} %reshape.95) | copy-start | bytes 5898244
  106.8 12.0 %slice-start.2 = ((s8[4718592]{0:T(1024)(128)(4,1)}), s8[4194304]{0:T(1024)(128)(4,1)S(1)}, s32[]{:S(2)}) async-start(s8[4718592]{0:T(1024)(128)(4,1)} %bitcast.63), calls=%async_computation.8 | async-start | bytes 8388608
  112.1 6.7 %copy-start.11 = (f32[640,1536]{1,0:T(8,128)}, f32[640,1536]{1,0:T(8,128)S(1)}, u32[]{:S(2)}) copy-start(f32[640,1536]{1,0:T(8,128)S(1)} %fusion.6) | copy-start | bytes 11796484
  112.1 6.7 %copy-start.3 = (bf16[640,1536]{1,0:T(8,128)(2,1)S(1)}, bf16[640,1536]{1,0:T(8,128)(2,1)}, u32[]{:S(2)}) copy-start(bf16[640,1536]{1,0:T(8,128)(2,1)} %reshape.93) | copy-start | bytes 5898244
  112.1 6.7 %slice-start.3 = ((s8[4718592]{0:T(1024)(128)(4,1)}), s8[524288]{0:T(1024)(128)(4,1)S(1)}, s32[]{:S(2)}) async-start(s8[4718592]{0:T(1024)(128)(4,1)} %bitcast.63), calls=%async_computation.9 | async-start | bytes 1048576
  118.8 5.4 %copy-start.9 = (f32[640,1536]{1,0:T(8,128)}, f32[640,1536]{1,0:T(8,128)S(1)}, u32[]{:S(2)}) copy-start(f32[640,1536]{1,0:T(8,128)S(1)} %fusion.2) | copy-start | bytes 11796484
  124.9 20.7 %all-to-all-start.3 = ((bf16[32,1,20]{2,1,0:T(2,128)(2,1)}), bf16[32,1,20]{2,1,0:T(2,128)(2,1)S(1)}, u32[]{:S(2)}, u32[]{:S(2)}) async-start(bf16[32,1,20]{2,1,0:T(2,128)(2,1)} %convert_element_type.97), calls=%async_computation.3 | async-start | bytes 32768 | tf_op jit(solution)/shard_map/all_to_all | solution.py:78
  128.8 9.0 %copy-start.10 = (f32[640,1536]{1,0:T(8,128)S(1)}, f32[640,1536]{1,0:T(8,128)}, u32[]{:S(2)}) copy-start(f32[640,1536]{1,0:T(8,128)} %copy-done.9) | copy-start | bytes 11796484
  128.8 9.0 %copy-start.13 = (f32[640,1536]{1,0:T(8,128)S(1)}, f32[640,1536]{1,0:T(8,128)}, u32[]{:S(2)}) copy-start(f32[640,1536]{1,0:T(8,128)} %get-tuple-element.12) | copy-start | bytes 11796484
  143.6 9.8 %copy-start.5 = (f32[128,4]{0,1:T(4,128)S(1)}, f32[128,4]{0,1:T(4,128)}, u32[]{:S(2)}) copy-start(f32[128,4]{0,1:T(4,128)} %param.11) | copy-start | bytes 6148
  145.7 38.9 %all-to-all-start.2 = ((bf16[32,20,1536]{2,1,0:T(8,128)(2,1)}), bf16[32,20,1536]{2,1,0:T(8,128)(2,1)S(1)}, u32[]{:S(2)}, u32[]{:S(2)}) async-start(bf16[32,20,1536]{2,1,0:T(8,128)(2,1)} %reshape.96), calls=%async_computation.2 | async-start | bytes 4718592 | tf_op jit(solution)/shard_map/all_to_all | solution.py:78
  186.1 9.9 %copy-start.6 = (bf16[2560,1536]{1,0:T(8,128)(2,1)S(1)}, bf16[2560,1536]{1,0:T(8,128)(2,1)}, u32[]{:S(2)}) copy-start(bf16[2560,1536]{1,0:T(8,128)(2,1)} %all-gather.5.cloned.1.call-done) | copy-start | bytes 23592964
  220.3 7.4 %copy-start.7 = (bf16[2560,1536]{1,0:T(8,128)(2,1)S(1)}, bf16[2560,1536]{1,0:T(8,128)(2,1)}, u32[]{:S(2)}) copy-start(bf16[2560,1536]{1,0:T(8,128)(2,1)} %all-gather.5.cloned.1.call-done) | copy-start | bytes 23592964
  220.3 7.4 %copy-start.8 = (f32[2560,384]{1,0:T(8,128)S(1)}, f32[2560,384]{1,0:T(8,128)}, u32[]{:S(2)}) copy-start(f32[2560,384]{1,0:T(8,128)} %fusion.25) | copy-start | bytes 11796484
  227.7 4.5 %copy-start.12 = (f32[2560,384]{1,0:T(8,128)S(1)}, f32[2560,384]{1,0:T(8,128)}, u32[]{:S(2)}) copy-start(f32[2560,384]{1,0:T(8,128)} %convolution_add_fusion) | copy-start | bytes 11796484
  227.7 9.0 %slice-start = ((s8[7864320]{0:T(1024)(128)(4,1)}), s8[4194304]{0:T(1024)(128)(4,1)S(1)}, s32[]{:S(2)}) async-start(s8[7864320]{0:T(1024)(128)(4,1)} %bitcast.61), calls=%async_computation.6 | async-start | bytes 8388608
  232.2 4.6 %slice-start.1 = ((s8[7864320]{0:T(1024)(128)(4,1)}), s8[3670016]{0:T(1024)(128)(4,1)S(1)}, s32[]{:S(2)}) async-start(s8[7864320]{0:T(1024)(128)(4,1)} %bitcast.61), calls=%async_computation.7 | async-start | bytes 7340032
  236.7 4.4 %copy-start.1 = (bf16[128,1536]{1,0:T(8,128)(2,1)S(1)}, bf16[128,1536]{1,0:T(8,128)(2,1)}, u32[]{:S(2)}) copy-start(bf16[128,1536]{1,0:T(8,128)(2,1)} %param.10) | copy-start | bytes 1179652
Sparse Core Ops, SparseCore 0:
  62.9 76.0 all-gather.4
  140.7 79.5 all-gather.2
where the time goes:
time: 249 us; the launch traced here: 248 us
  matrix products  76.9 us (31%)
  blocking collectives  75.7 us (30%)
  waiting for transfers between devices  47.5 us (19%)
  local copies, waits for them, and re-layouts  16.4 us (7%)
  between operations  14.4 us (6%)
  starting transfers between devices  11.2 us (4%)
  other arithmetic  5.9 us (2%)
    all_to_all x2, blocking collectives, exchange(): return lax.all_to_all(a, 'ep', split_axis=0, concat_axis=0, tiled=True)  75.7 us
    dot_general x6, matrix products, contract_last(): lax.dot_general(first_op, second_op, (((1,), (1,)), ((), ())), preferred_...  42 us
    all_to_all x2, waiting for transfers between devices, exchange(): return lax.all_to_all(a, 'ep', split_axis=0, concat_axis=0, tiled=True)  30.6 us
    all_gather x1, waiting for transfers between devices, on_device(): all_g = lax.all_gather(slot_g, 'dp', axis=0, tiled=True)  16.9 us
    dot_general x3, matrix products, contract_first(): lax.dot_general(first_op, second_op, (((0,), (0,)), ((), ())), preferred_...  13.4 us
    all_to_all x2, starting transfers between devices, exchange(): return lax.all_to_all(a, 'ep', split_axis=0, concat_axis=0, tiled=True)  11.1 us
    dot_general x1, matrix products, on_device(): jnp.dot(gate_delta, w_gate, preferred_element_type=jnp.float32)  8.95 us
    dot_general x1, matrix products, on_device(): jnp.dot(up_delta, w_up, preferred_element_type=jnp.float32)  5.8 us
  transfers between devices with their start and end apart: 4, of which 2 were waited for; matrix products, arithmetic and copies ran while one was open for 26% of the time, Pallas kernels for 0%

commit v1 on v0

--- a/solution.py
+++ b/solution.py
@@ -2,6 +2,7 @@
 import jax.numpy as jnp
 from jax import lax
 from jax.sharding import PartitionSpec as P
+from jax.lax import all_gather
 
 sharpness = 1.702
 
@@ -78,9 +79,14 @@
         return lax.all_to_all(a, "ep", split_axis=0, concat_axis=0, tiled=True)
 
     slot_x = exchange(send_x.reshape(bucket_shape)).reshape(slot_rows, model_width)
-    all_x = lax.all_gather(slot_x, "dp", axis=0, tiled=True)
     slot_g = exchange(send_g.reshape(bucket_shape)).reshape(slot_rows, model_width)
-    all_g = lax.all_gather(slot_g, "dp", axis=0, tiled=True)
+
+    def supply_orders(local, vec):
+        ready = jnp.concatenate([local, vec], axis=1)
+        part_next = all_gather(ready, axis=0, tiled=True, axis_name="dp")
+        return jnp.split(part_next, [local.shape[1]], axis=1)
+
+    all_x, all_g = supply_orders(slot_x, vec=slot_g)
     w_gate = gate_weight[0]
     w_up = up_weight[0]
     w_down = down_weight[0]

time: 249 us -> 294 us (1.18)
  waiting for transfers between devices: 47.5 us -> 146 us
  blocking collectives: 75.7 us -> 0 us
  starting transfers between devices: 11.2 us -> 29 us
  other arithmetic: 5.9 us -> 9.78 us
    all_to_all x2 -> x0, blocking collectives: 75.7 us -> none  [exchange(): return lax.all_to_all(a, 'ep', split_axis=0, concat_axis=0, tiled=True)]
    all_to_all x2 -> x4, waiting for transfers between devices: 30.6 us -> 83.9 us  [exchange(): return lax.all_to_all(a, 'ep', split_axis=0, concat_axis=0, tiled=True)]
    all_gather x2 -> x1, waiting for transfers between devices: 16.9 us -> 62.2 us  [supply_orders(): part_next = all_gather(ready, axis=0, tiled=True, axis_name='dp')]
    all_to_all x2 -> x4, starting transfers between devices: 11.1 us -> 29 us  [exchange(): return lax.all_to_all(a, 'ep', split_axis=0, concat_axis=0, tiled=True)]
    dot_general x3, matrix products: 13.4 us -> 18.8 us  [contract_first(): lax.dot_general(first_op, second_op, (((0,), (0,)), ((), ())), preferred_...]
    dot_general x6, matrix products: 42 us -> 38 us  [contract_last(): lax.dot_general(first_op, second_op, (((1,), (1,)), ((), ())), preferred_...]
    concatenate x0 -> x1, other arithmetic: none -> 3.87 us  [supply_orders(): ready = jnp.concatenate([local, vec], axis=1)]
  transfers between devices with their start and end apart: 4 -> 5, of which waited for: 2 -> 4; matrix products, arithmetic and copies ran while one was open for 26% -> 16% of each run, Pallas kernels for 0% -> 0%
where the time goes in v1:
time: 294 us
  waiting for transfers between devices  146 us (50%)
  matrix products  78.2 us (27%)
  starting transfers between devices  29 us (10%)
  local copies, waits for them, and re-layouts  16.1 us (5%)
  between operations  14.3 us (5%)
  other arithmetic  9.78 us (3%)
    all_to_all x4, waiting for transfers between devices, exchange(): return lax.all_to_all(a, 'ep', split_axis=0, concat_axis=0, tiled=True)  83.9 us
    all_gather x1, waiting for transfers between devices, supply_orders(): part_next = all_gather(ready, axis=0, tiled=True, axis_name='dp')  62.2 us
    dot_general x6, matrix products, contract_last(): lax.dot_general(first_op, second_op, (((1,), (1,)), ((), ())), preferred_...  38 us
    all_to_all x4, starting transfers between devices, exchange(): return lax.all_to_all(a, 'ep', split_axis=0, concat_axis=0, tiled=True)  29 us
    dot_general x3, matrix products, contract_first(): lax.dot_general(first_op, second_op, (((0,), (0,)), ((), ())), preferred_...  18.8 us
    dot_general x1, matrix products, on_device(): jnp.dot(gate_delta, w_gate, preferred_element_type=jnp.float32)  8.99 us
  transfers between devices with their start and end apart: 5, of which 4 were waited for; matrix products, arithmetic and copies ran while one was open for 16% of the time, Pallas kernels for 0%

profile of v1, /device:TPU:1, one launch (start us, length us, event | category | flops | bytes accessed | tf_op | source)
XLA Modules:
  0.0 293.5 jit_solution(14144640980499221936)
XLA Ops:
  14.2 2.1 reshape.94
  16.3 9.4 %all-to-all-start.1 = ((bf16[32,20,1536]{2,1,0:T(8,128)(2,1)}), bf16[32,20,1536]{2,1,0:T(8,128)(2,1)S(1)}, u32[]{:S(2)}, u32[]{:S(2)}) async-start(bf16[32,20,1536]{2,1,0:T(8,128)(2,1)} %reshape.94), calls=%async_computation.1 | async-start | bytes 4718592 | tf_op jit(solution)/shard_map/all_to_all | solution.py:79
  26.0 3.2 %multiply_convert_fusion.5 = bf16[640,1536]{1,0:T(8,128)(2,1)} fusion(bf16[128,640]{0,1:T(8,128)(2,1)S(1)} %convert_element_type.81, f32[640]{0:T(1024)S(1)} %mul.136, f32[128,1536]{1,0:T(8,128)} %param.9, f32[128]{0:T(128)S(1)} %broadcast_maximum_fusion), kind=kOutput, calls=%fused_computation.33 | convolution fusion | flops 254017536 | bytes 2919424 | tf_op jit(solution)/shard_map/ts,td->sd/dot_general | solution.py:73
  29.2 4.0 %reshape.92 = bf16[32,20,1536]{2,1,0:T(8,128)(2,1)} reshape(bf16[640,1536]{1,0:T(8,128)(2,1)} %multiply_convert_fusion.5) | data formatting | bytes 3932160 | tf_op jit(solution)/shard_map/reshape | solution.py:82
  33.1 24.1 %all-to-all-done.1 = bf16[32,20,1536]{2,1,0:T(8,128)(2,1)S(1)} async-done(((bf16[32,20,1536]{2,1,0:T(8,128)(2,1)}), bf16[32,20,1536]{2,1,0:T(8,128)(2,1)S(1)}, u32[]{:S(2)}, u32[]{:S(2)}) %all-to-all-start.1) | async-done | bytes 1966112 | tf_op jit(solution)/shard_map/all_to_all | solution.py:79
  57.3 6.3 %all-to-all-start = ((bf16[32,20,1536]{2,1,0:T(8,128)(2,1)}), bf16[32,20,1536]{2,1,0:T(8,128)(2,1)}, u32[]{:S(2)}, u32[]{:S(2)}) async-start(bf16[32,20,1536]{2,1,0:T(8,128)(2,1)} %reshape.92), calls=%async_computation | async-start | bytes 4718592 | tf_op jit(solution)/shard_map/all_to_all | solution.py:79
  65.6 29.2 %all-to-all-done = bf16[32,20,1536]{2,1,0:T(8,128)(2,1)} async-done(((bf16[32,20,1536]{2,1,0:T(8,128)(2,1)}), bf16[32,20,1536]{2,1,0:T(8,128)(2,1)}, u32[]{:S(2)}, u32[]{:S(2)}) %all-to-all-start) | async-done | bytes 1966112 | tf_op jit(solution)/shard_map/all_to_all | solution.py:79
  94.8 4.0 %reshape.93 = bf16[640,1536]{1,0:T(8,128)(2,1)} reshape(bf16[32,20,1536]{2,1,0:T(8,128)(2,1)} %all-to-all-done) | data formatting | bytes 3932160 | tf_op jit(solution)/shard_map/reshape | solution.py:82
  98.9 3.9 %pad_maximum_fusion = bf16[640,3072]{1,0:T(8,128)(2,1)} fusion(bf16[640,1536]{1,0:T(8,128)(2,1)} %reshape.93, bf16[640,1536]{1,0:T(8,128)(2,1)S(1)} %copy-done.2), kind=kLoop, calls=%fused_computation.23 | loop fusion | flops 7864320 | bytes 7864320 | tf_op jit(solution)/shard_map/concatenate | solution.py:85
  102.8 5.3 %fusion.18 = f32[640,1536]{1,0:T(8,128)S(1)} fusion(bf16[640,1536]{1,0:T(8,128)(2,1)S(1)} %copy-done.2, bf16[1,1536,1536]{2,1,0:T(8,128)(2,1)} %param.16), kind=kOutput, calls=%fused_computation.18 | convolution fusion | flops 3019898880 | bytes 10616832 | tf_op jit(solution)/shard_map/dot_general | solution.py:11
  108.1 6.7 %fusion.14 = f32[640,1536]{1,0:T(8,128)S(1)} fusion(bf16[640,1536]{1,0:T(8,128)(2,1)S(1)} %copy-done.2, bf16[1,1536,1536]{2,1,0:T(8,128)(2,1)} %param.15), kind=kOutput, calls=%fused_computation.14 | convolution fusion | flops 3019898880 | bytes 10616832 | tf_op jit(solution)/shard_map/dot_general | solution.py:11
  114.9 5.5 %multiply_reduce_fusion = (bf16[640]{0:T(1024)(128)(2,1)S(1)}, f32[640,1536]{1,0:T(8,128)}) fusion(f32[640,1536]{1,0:T(8,128)S(1)} %fusion.18, f32[640,1536]{1,0:T(8,128)S(1)} %fusion.14, bf16[640,1536]{1,0:T(8,128)(2,1)S(1)} %copy-done.3, bf16[1,1536,1536]{2,1,0:T(8,128)(2,1)S(1)} %bitcast.56), kind=kOutput, calls=%fused_computation.28 | convolution fusion | flops 3028745728 | bytes 18482432 | tf_op jit(solution)/shard_map/dot_general | solution.py:11
  121.1 5.8 %all-to-all-start.3 = ((bf16[32,1,20]{2,1,0:T(2,128)(2,1)}), bf16[32,1,20]{2,1,0:T(2,128)(2,1)S(1)}, u32[]{:S(2)}, u32[]{:S(2)}) async-start(bf16[32,1,20]{2,1,0:T(2,128)(2,1)} %convert_element_type.97), calls=%async_computation.3 | async-start | bytes 32768 | tf_op jit(solution)/shard_map/all_to_all | solution.py:79
  126.9 9.0 %fusion.12 = f32[640,1536]{1,0:T(8,128)S(1)} fusion(bf16[1,1536,1536]{2,1,0:T(8,128)(2,1)} %param.15, f32[640,1536]{1,0:T(8,128)} %get-tuple-element.12, f32[640,1536]{1,0:T(8,128)} %copy-done.6, f32[640,1536]{1,0:T(8,128)} %copy-done.8), kind=kOutput, calls=%fused_computation.12 | convolution fusion | flops 3031695360 | bytes 20447232 | tf_op jit(solution)/shard_map/dot_general | solution.py:95
  135.9 5.8 %add_convert_fusion = bf16[640,1536]{1,0:T(8,128)(2,1)S(1)} fusion(f32[640,1536]{1,0:T(8,128)S(1)} %fusion.12, bf16[1,1536,1536]{2,1,0:T(8,128)(2,1)} %param.16, f32[640,1536]{1,0:T(8,128)S(1)} %copy-done.9, f32[640,1536]{1,0:T(8,128)S(1)} %copy-done.7), kind=kOutput, calls=%fused_computation.29 | convolution fusion | flops 3028746240 | bytes 18481152 | tf_op jit(solution)/shard_map/dot_general | solution.py:96
  143.8 7.5 %all-to-all-start.2 = ((bf16[32,20,1536]{2,1,0:T(8,128)(2,1)}), bf16[32,20,1536]{2,1,0:T(8,128)(2,1)S(1)}, u32[]{:S(2)}, u32[]{:S(2)}) async-start(bf16[32,20,1536]{2,1,0:T(8,128)(2,1)} %reshape.96), calls=%async_computation.2 | async-start | bytes 4718592 | tf_op jit(solution)/shard_map/all_to_all | solution.py:79
  152.2 30.6 %all-to-all-done.2 = bf16[32,20,1536]{2,1,0:T(8,128)(2,1)S(1)} async-done(((bf16[32,20,1536]{2,1,0:T(8,128)(2,1)}), bf16[32,20,1536]{2,1,0:T(8,128)(2,1)S(1)}, u32[]{:S(2)}, u32[]{:S(2)}) %all-to-all-start.2) | async-done | bytes 1966112 | tf_op jit(solution)/shard_map/all_to_all | solution.py:79
  184.4 62.2 %all-gather.2.cloned.1.call-done = bf16[2560,3072]{1,0:T(8,128)(2,1)} async-done(((bf16[640,3072]{1,0:T(8,128)(2,1)}), bf16[2560,3072]{1,0:T(8,128)(2,1)}) %all-gather.2.cloned.1.call-update) | async-done | bytes 15728656 | tf_op jit(solution)/shard_map/all_gather | solution.py:86
  246.5 7.4 %fusion.2 = f32[2560,384]{1,0:T(8,128)S(1)} fusion(bf16[2560,3072]{1,0:T(8,128)(2,1)} %all-gather.2.cloned.1.call-done, bf16[1,1536,1536]{2,1,0:T(8,128)(2,1)} %param.17, s32[]{:T(128)S(6)} %select_n.2), kind=kOutput, calls=%fused_computation.2 | convolution fusion | flops 3019898880 | bytes 12976132 | tf_op jit(solution)/shard_map/dot_general | solution.py:11
  254.7 7.6 %fusion.22 = f32[2560,384]{1,0:T(8,128)} fusion(bf16[2560,3072]{1,0:T(8,128)(2,1)S(1)} %copy-done.5, bf16[1,1536,1536]{2,1,0:T(8,128)(2,1)} %param.16, s32[]{:T(128)S(6)} %select_n.2), kind=kOutput, calls=%fused_computation.22 | convolution fusion | flops 3020881920 | bytes 12976132 | tf_op jit(solution)/shard_map/dot_general | solution.py:11
  262.3 5.6 %fusion.8 = f32[2560,384]{1,0:T(8,128)S(1)} fusion(bf16[2560,3072]{1,0:T(8,128)(2,1)S(1)} %copy-done.5, bf16[1,1536,1536]{2,1,0:T(8,128)(2,1)} %param.15, s32[]{:T(128)S(6)} %select_n.2), kind=kOutput, calls=%fused_computation.8 | convolution fusion | flops 3019898880 | bytes 12976132 | tf_op jit(solution)/shard_map/dot_general | solution.py:11
  267.8 4.6 %fusion.41 = bf16[1,384,1536]{2,1,0:T(8,128)(2,1)} fusion(bf16[2560,3072]{1,0:T(8,128)(2,1)S(1)} %copy-done.5, f32[2560,384]{1,0:T(8,128)S(1)} %fusion.2, f32[2560,384]{1,0:T(8,128)S(1)} %fusion.8), kind=kOutput, calls=%fused_computation.41 | convolution fusion | flops 3027369984 | bytes 16908288 | tf_op jit(solution)/shard_map/dot_general | solution.py:17
  272.5 7.4 %fusion.44 = bf16[1,384,1536]{2,1,0:T(8,128)(2,1)} fusion(bf16[2560,3072]{1,0:T(8,128)(2,1)S(1)} %copy-done.5, f32[2560,384]{1,0:T(8,128)S(1)} %fusion.2, f32[2560,384]{1,0:T(8,128)} %fusion.22, f32[2560,384]{1,0:T(8,128)S(1)} %fusion.8), kind=kOutput, calls=%fused_computation.42 | convolution fusion | flops 3031302144 | bytes 20840448 | tf_op jit(solution)/shard_map/dot_general | solution.py:17
  279.9 6.8 %fusion.38 = bf16[1,384,1536]{2,1,0:T(8,128)(2,1)} fusion(bf16[2560,3072]{1,0:T(8,128)(2,1)S(1)} %copy-done.5, f32[2560,384]{1,0:T(8,128)} %fusion.22, f32[2560,384]{1,0:T(8,128)S(1)} %fusion.8), kind=kOutput, calls=%fused_computation.40 | convolution fusion | flops 3027369984 | bytes 16908288 | tf_op jit(solution)/shard_map/dot_general | solution.py:17
  (52 shorter events, 15.3 us)
Async XLA Ops:
  7.2 6.4 %copy-start = (bf16[128,1536]{1,0:T(8,128)(2,1)S(1)}, bf16[128,1536]{1,0:T(8,128)(2,1)}, u32[]{:S(2)}) copy-start(bf16[128,1536]{1,0:T(8,128)(2,1)} %param.10) | copy-start | bytes 1179652
  16.3 40.9 %all-to-all-start.1 = ((bf16[32,20,1536]{2,1,0:T(8,128)(2,1)}), bf16[32,20,1536]{2,1,0:T(8,128)(2,1)S(1)}, u32[]{:S(2)}, u32[]{:S(2)}) async-start(bf16[32,20,1536]{2,1,0:T(8,128)(2,1)} %reshape.94), calls=%async_computation.1 | async-start | bytes 4718592 | tf_op jit(solution)/shard_map/all_to_all | solution.py:79
  57.3 37.6 %all-to-all-start = ((bf16[32,20,1536]{2,1,0:T(8,128)(2,1)}), bf16[32,20,1536]{2,1,0:T(8,128)(2,1)}, u32[]{:S(2)}, u32[]{:S(2)}) async-start(bf16[32,20,1536]{2,1,0:T(8,128)(2,1)} %reshape.92), calls=%async_computation | async-start | bytes 4718592 | tf_op jit(solution)/shard_map/all_to_all | solution.py:79
  63.5 183.0 %all-gather.2.cloned.1.call-start = ((), (), s32[]{:S(2)}) async-start(), calls=%async_computation.4 | async-start | bytes 19660800 | tf_op jit(solution)/shard_map/all_gather | solution.py:86
  65.6 33.2 %copy-start.2 = (bf16[640,1536]{1,0:T(8,128)(2,1)S(1)}, bf16[640,1536]{1,0:T(8,128)(2,1)}, u32[]{:S(2)}) copy-start(bf16[640,1536]{1,0:T(8,128)(2,1)} %reshape.95) | copy-start | bytes 5898244
  102.8 12.1 %slice-start = ((s8[4718592]{0:T(1024)(128)(4,1)}), s8[4194304]{0:T(1024)(128)(4,1)S(1)}, s32[]{:S(2)}) async-start(s8[4718592]{0:T(1024)(128)(4,1)} %bitcast.55), calls=%async_computation.5 | async-start | bytes 8388608
  108.1 6.8 %copy-start.8 = (f32[640,1536]{1,0:T(8,128)}, f32[640,1536]{1,0:T(8,128)S(1)}, u32[]{:S(2)}) copy-start(f32[640,1536]{1,0:T(8,128)S(1)} %fusion.18) | copy-start | bytes 11796484
  108.1 6.8 %copy-start.3 = (bf16[640,1536]{1,0:T(8,128)(2,1)S(1)}, bf16[640,1536]{1,0:T(8,128)(2,1)}, u32[]{:S(2)}) copy-start(bf16[640,1536]{1,0:T(8,128)(2,1)} %reshape.93) | copy-start | bytes 5898244
  108.1 6.8 %slice-start.1 = ((s8[4718592]{0:T(1024)(128)(4,1)}), s8[524288]{0:T(1024)(128)(4,1)S(1)}, s32[]{:S(2)}) async-start(s8[4718592]{0:T(1024)(128)(4,1)} %bitcast.55), calls=%async_computation.6 | async-start | bytes 1048576
  114.9 5.5 %copy-start.6 = (f32[640,1536]{1,0:T(8,128)}, f32[640,1536]{1,0:T(8,128)S(1)}, u32[]{:S(2)}) copy-start(f32[640,1536]{1,0:T(8,128)S(1)} %fusion.14) | copy-start | bytes 11796484
  121.1 22.7 %all-to-all-start.3 = ((bf16[32,1,20]{2,1,0:T(2,128)(2,1)}), bf16[32,1,20]{2,1,0:T(2,128)(2,1)S(1)}, u32[]{:S(2)}, u32[]{:S(2)}) async-start(bf16[32,1,20]{2,1,0:T(2,128)(2,1)} %convert_element_type.97), calls=%async_computation.3 | async-start | bytes 32768 | tf_op jit(solution)/shard_map/all_to_all | solution.py:79
  126.9 9.0 %copy-start.7 = (f32[640,1536]{1,0:T(8,128)S(1)}, f32[640,1536]{1,0:T(8,128)}, u32[]{:S(2)}) copy-start(f32[640,1536]{1,0:T(8,128)} %copy-done.6) | copy-start | bytes 11796484
  126.9 9.0 %copy-start.9 = (f32[640,1536]{1,0:T(8,128)S(1)}, f32[640,1536]{1,0:T(8,128)}, u32[]{:S(2)}) copy-start(f32[640,1536]{1,0:T(8,128)} %get-tuple-element.12) | copy-start | bytes 11796484
  141.7 9.9 %copy-start.4 = (f32[128,4]{0,1:T(4,128)S(1)}, f32[128,4]{0,1:T(4,128)}, u32[]{:S(2)}) copy-start(f32[128,4]{0,1:T(4,128)} %param.11) | copy-start | bytes 6148
  143.8 39.0 %all-to-all-start.2 = ((bf16[32,20,1536]{2,1,0:T(8,128)(2,1)}), bf16[32,20,1536]{2,1,0:T(8,128)(2,1)S(1)}, u32[]{:S(2)}, u32[]{:S(2)}) async-start(bf16[32,20,1536]{2,1,0:T(8,128)(2,1)} %reshape.96), calls=%async_computation.2 | async-start | bytes 4718592 | tf_op jit(solution)/shard_map/all_to_all | solution.py:79
  246.5 8.1 %copy-start.5 = (bf16[2560,3072]{1,0:T(8,128)(2,1)S(1)}, bf16[2560,3072]{1,0:T(8,128)(2,1)}, u32[]{:S(2)}) copy-start(bf16[2560,3072]{1,0:T(8,128)(2,1)} %all-gather.2.cloned.1.call-done) | copy-start | bytes 47185924
  279.9 6.8 %copy-start.1 = (bf16[128,1536]{1,0:T(8,128)(2,1)S(1)}, bf16[128,1536]{1,0:T(8,128)(2,1)}, u32[]{:S(2)}) copy-start(bf16[128,1536]{1,0:T(8,128)(2,1)} %param.10) | copy-start | bytes 1179652
Sparse Core Ops, SparseCore 0:
  102.9 143.5 all-gather.1
